TPU v7x, 32 devices: a whole 2x2x4 slice. The times are simulated.
32 devices in a mesh: gx: 4 (over y, core), gy: 2 (over x), gz: 4 (over z).
Axes of the slice: x: 2, y: 2, z: 4, core: 2. Of those that a mesh axis runs over, the one named last changes fastest.
Arguments:
- tokens: bfloat16 [32, 6144], P('gy'), may hold values from -6 to 6
- route: int32 [32, 2], P('gy'), may hold values from 0 to 3, all different within a row; in each aligned block of 16 rows (0 to 15, 16 to 31, ...) at most 12 rows name the same one
- weight_q: int32 [32, 2], P('gy'), may hold values from 1 to 65535
- w_gate: bfloat16 [4, 6144, 16384], P('gx', 'gy', 'gz'), may hold values from -0.078125 to 0.078125
- w_up: bfloat16 [4, 6144, 16384], P('gx', 'gy', 'gz'), may hold values from -0.078125 to 0.078125
- w_down: bfloat16 [4, 16384, 6144], P('gx', 'gz', 'gy'), may hold values from -0.046875 to 0.046875
Outputs:
- mixed: bfloat16 [32, 6144], P('gy', ('gx', 'gz'))
Inputs may be any that keep to these rules, and one draw needn't show every extreme that they name: `route`: the 2 entries of a row are different; in each block of 16 rows owned by one index of gy no expert is named by more than 12 rows, a bound that some block reaches.
All inputs are finite; a program needn't handle non-finite values.
Results may differ from a plain program's by a relative error of at most 0.0049.
Values may be sent and summed in bfloat16 or wider, within the bound.
A program may use at most 256 MiB of HBM per device.

v0:
```python
import jax
import jax.numpy as jnp
from jax import lax
from jax.sharding import PartitionSpec as P

CAP = 12


def per_device(tokens, route, weight_q, w_gate, w_up, w_down):
    expert = lax.axis_index("gx")
    width_z = lax.axis_size("gz")
    owners = lax.axis_size("gy")
    hits = (route == expert).astype(jnp.int32)
    routed = jnp.sum(hits, axis=1)
    slot_index = jnp.cumsum(routed) - 1
    columns = jnp.arange(CAP, dtype=jnp.int32)
    placing = (slot_index[None, :] == columns[:, None]) & (routed[None, :] > 0)
    place_half = placing.astype(jnp.bfloat16)
    place_full = placing.astype(jnp.float32)
    outgoing = jnp.dot(place_half, tokens, preferred_element_type=jnp.float32).astype(jnp.bfloat16)
    weights_f = weight_q.astype(jnp.float32)
    shares = weights_f / jnp.sum(weights_f, axis=1, keepdims=True)
    token_gate = jnp.sum(hits.astype(jnp.float32) * shares, axis=1)
    slot_gate = jnp.dot(place_full, token_gate, precision=lax.Precision.HIGHEST)
    gate_slab, up_slab = (
        lax.all_to_all(w_gate[0], "gy", split_axis=1, concat_axis=0, tiled=True),
        lax.all_to_all(w_up[0], "gy", split_axis=1, concat_axis=0, tiled=True),
    )
    piece = lax.all_gather(outgoing, "gy", axis=0, tiled=True)
    gate = jnp.dot(piece, gate_slab, preferred_element_type=jnp.float32)
    upper = jnp.dot(piece, up_slab, preferred_element_type=jnp.float32)
    hidden = (jax.nn.silu(gate) * upper).astype(jnp.bfloat16)
    down_local = w_down[0]
    partial_value = jnp.dot(
        lax.all_gather(hidden, "gy", axis=1, tiled=True),
        down_local,
        preferred_element_type=jnp.float32,
    )
    portion = CAP // width_z
    column_width = partial_value.shape[1]
    blocks = partial_value.reshape(owners, width_z, portion, column_width)
    narrowed = lax.psum_scatter(blocks, "gz", scatter_dimension=1, tiled=True)
    arrived = lax.all_to_all(narrowed, "gy", split_axis=0, concat_axis=1, tiled=True)
    full = jnp.transpose(arrived[0], (1, 0, 2)).reshape(portion, owners * column_width)
    first = lax.axis_index("gz") * portion
    gate_part = lax.dynamic_slice_in_dim(slot_gate, first, portion, 0)
    place_part = lax.dynamic_slice_in_dim(place_full, first, portion, 0)
    weighted = gate_part[:, None] * full
    contribution = jnp.dot(place_part.T, weighted, precision=lax.Precision.HIGHEST)
    result = lax.psum_scatter(contribution, ("gx", "gz"), scatter_dimension=1, tiled=True)
    return result.astype(jnp.bfloat16)


def solution(mesh):
    in_specs = (
        P("gy", None),
        P("gy", None),
        P("gy", None),
        P("gx", "gy", "gz"),
        P("gx", "gy", "gz"),
        P("gx", "gz", "gy"),
    )
    out_specs = P("gy", ("gx", "gz"))
    return jax.shard_map(
        per_device, mesh=mesh, in_specs=in_specs, out_specs=out_specs, check_vma=False
    )
```

profile of v0, /device:TPU:0, one launch (start us, length us, event | category | flops | bytes accessed | tf_op | source)
XLA Modules:
  0.0 822.6 jit_solution(7426309213816833088)
XLA Ops:
  6.5 0.0 copy-start
  6.5 32.7 %copy.36 = bf16[1,3072,4096]{1,2,0:T(8,128)(2,1)} copy(bf16[1,3072,4096]{2,1,0:T(8,128)(2,1)} %param.9) | data formatting | bytes 50331648 | tf_op args[3]
  39.2 11.8 %all-to-all-start = ((bf16[3072,2,2048]{0,2,1:T(8,128)(2,1)}), bf16[3072,2,2048]{0,2,1:T(8,128)(2,1)}, u32[]{:S(2)}, u32[]{:S(2)}) async-start(bf16[3072,2,2048]{0,2,1:T(8,128)(2,1)} %bitcast.37), calls=%async_computation | async-start | bytes 50331648 | tf_op jit(solution)/shard_map/all_to_all | solution.py:26
  51.0 32.7 %copy.38 = bf16[1,3072,4096]{1,2,0:T(8,128)(2,1)} copy(bf16[1,3072,4096]{2,1,0:T(8,128)(2,1)} %param.10) | data formatting | bytes 50331648 | tf_op args[4]
  83.7 240.8 %all-to-all-done = bf16[3072,2,2048]{0,2,1:T(8,128)(2,1)} async-done(((bf16[3072,2,2048]{0,2,1:T(8,128)(2,1)}), bf16[3072,2,2048]{0,2,1:T(8,128)(2,1)}, u32[]{:S(2)}, u32[]{:S(2)}) %all-to-all-start) | async-done | bytes 25165856 | tf_op jit(solution)/shard_map/all_to_all | solution.py:26
  324.5 0.0 copy-start.2
  324.5 0.0 copy-start.4
  324.5 0.0 copy-start.3
  324.5 11.9 %all-to-all-start.1 = ((bf16[3072,2,2048]{0,2,1:T(8,128)(2,1)}), bf16[3072,2,2048]{0,2,1:T(8,128)(2,1)}, u32[]{:S(2)}, u32[]{:S(2)}) async-start(bf16[3072,2,2048]{0,2,1:T(8,128)(2,1)} %bitcast.36), calls=%async_computation.1 | async-start | bytes 50331648 | tf_op jit(solution)/shard_map/all_to_all | solution.py:27
  336.5 0.0 all-reduce.3.cloned.1.call-start
  336.5 0.0 copy-done.2
  336.6 0.1 copy.35
  336.7 0.1 add_reduce_fusion
  336.8 0.0 copy-done
  336.8 0.2 fusion.2
  337.0 275.4 %all-gather = bf16[2,12,6144]{2,1,0:T(8,128)(2,1)S(1)} all-gather(bf16[1,12,6144]{2,1,0:T(8,128)(2,1)S(1)} %fusion.2), channel_id=1, replica_groups=mesh['gx'=4,'gy'=2,'gz'=4] {'gy'}, dimensions={0}, use_global_device_ids=true | all-gather | bytes 442368 | tf_op jit(solution)/shard_map/all_gather | solution.py:29
  612.4 0.1 reshape.53
  612.5 0.0 copy-done.4
  612.5 0.6 dynamic-slice
  613.1 0.0 copy-done.3
  613.1 31.6 %copy.37 = bf16[2,3072,2048]{2,1,0:T(8,128)(2,1)} copy(bf16[2,3072,2048]{1,2,0:T(8,128)(2,1)} %bitcast.5) | data formatting | bytes 50331648 | tf_op jit(solution)/shard_map/all_to_all | solution.py:26
  644.7 0.0 all-to-all-done.1
  644.7 32.7 %copy.39 = bf16[2,3072,2048]{2,1,0:T(8,128)(2,1)} copy(bf16[2,3072,2048]{1,2,0:T(8,128)(2,1)} %bitcast.8) | data formatting | bytes 50331648 | tf_op jit(solution)/shard_map/all_to_all | solution.py:27
  677.4 9.9 %fusion.16 = f32[24,2048]{1,0:T(8,128)S(1)} fusion(bf16[24,6144]{1,0:T(8,128)(2,1)S(1)} %reshape.53, bf16[6144,2048]{1,0:T(8,128)(2,1)} %bitcast.34), kind=kOutput, calls=%fused_computation.25 | convolution fusion | flops 603979776 | bytes 25657344 | tf_op jit(solution)/shard_map/dot_general | solution.py:30
  687.3 0.0 copy-start.1
  687.3 10.0 %fusion.3 = bf16[24,2048]{1,0:T(8,128)(2,1)S(1)} fusion(bf16[24,6144]{1,0:T(8,128)(2,1)S(1)} %reshape.53, bf16[6144,2048]{1,0:T(8,128)(2,1)} %bitcast.35, f32[24,2048]{1,0:T(8,128)S(1)} %fusion.16), kind=kOutput, calls=%fused_computation.5 | convolution fusion | flops 604274688 | bytes 25755648 | tf_op jit(solution)/shard_map/dot_general | solution.py:31
  697.3 5.3 all_gather.7
  702.6 0.1 dot_general.24
  702.8 11.3 %fusion = f32[2,4,3,3072]{3,0,2,1:T(2,128)} fusion(bf16[1,4096,3072]{2,1,0:T(8,128)(2,1)} %param.11, bf16[2,4,3,4096]{3,2,1,0:T(4,128)(2,1)S(1)} %dot_general.24), kind=kOutput, calls=%fused_computation | convolution fusion | flops 603979776 | bytes 25657344 | tf_op jit(solution)/shard_map/dot_general | solution.py:34
  714.1 0.0 all-reduce.3.cloned.1.call-update
  714.1 36.5 %all-reduce.3.cloned.1.call-done = f32[2,4,3,3072]{3,0,2,1:T(2,128)} async-done(((f32[2,4,3,3072]{3,0,2,1:T(2,128)}), f32[2,4,3,3072]{3,0,2,1:T(2,128)}) %all-reduce.3.cloned.1.call-update) | async-done | bytes 294928
  750.6 1.5 constant_dynamic-slice_fusion
  752.1 0.7 copy.42
  752.8 3.3 all-to-all-start.2
  756.1 0.0 reduce-scatter.2.cloned.1.call-start
  756.2 0.1 convolution_bitcast_fusion
  756.3 0.1 dynamic_slice.7
  756.4 3.9 all-to-all-done.2
  760.4 1.2 fusion.5
  761.6 0.0 reduce-scatter.2.cloned.1.call-update
  761.6 52.8 %reduce-scatter.2.cloned.1.call-done = f32[16,384]{1,0:T(8,128)} async-done(((f32[16,6144]{1,0:T(8,128)}), f32[16,384]{1,0:T(8,128)}) %reduce-scatter.2.cloned.1.call-update) | async-done | bytes 24592 | tf_op jit(solution)/shard_map/reduce_scatter | solution.py:50
  814.4 1.3 convert_element_type.25
  815.8 0.0 copy-done.1
  (8 shorter events, 0.2 us)
Async XLA Ops:
  6.5 330.3 %copy-start = (bf16[16,6144]{1,0:T(8,128)(2,1)S(1)}, bf16[16,6144]{1,0:T(8,128)(2,1)}, u32[]{:S(2)}) copy-start(bf16[16,6144]{1,0:T(8,128)(2,1)} %param.6) | copy-start | bytes 589828
  39.2 285.3 %all-to-all-start = ((bf16[3072,2,2048]{0,2,1:T(8,128)(2,1)}), bf16[3072,2,2048]{0,2,1:T(8,128)(2,1)}, u32[]{:S(2)}, u32[]{:S(2)}) async-start(bf16[3072,2,2048]{0,2,1:T(8,128)(2,1)} %bitcast.37), calls=%async_computation | async-start | bytes 50331648 | tf_op jit(solution)/shard_map/all_to_all | solution.py:26
  324.5 12.0 %copy-start.2 = (s32[16,2]{0,1:T(2,128)S(1)}, s32[16,2]{0,1:T(2,128)}, u32[]{:S(2)}) copy-start(s32[16,2]{0,1:T(2,128)} %param.7) | copy-start | bytes 388
  324.5 288.0 %copy-start.4 = (u32[32]{0:T(128)S(1)}, u32[32]{0:T(128)}, u32[]{:S(2)}) copy-start(u32[32]{0:T(128)} %constant.30) | copy-start | bytes 388
  324.5 288.5 %copy-start.3 = (s32[16,2]{0,1:T(2,128)S(1)}, s32[16,2]{0,1:T(2,128)}, u32[]{:S(2)}) copy-start(s32[16,2]{0,1:T(2,128)} %param.8) | copy-start | bytes 388
  324.5 320.2 %all-to-all-start.1 = ((bf16[3072,2,2048]{0,2,1:T(8,128)(2,1)}), bf16[3072,2,2048]{0,2,1:T(8,128)(2,1)}, u32[]{:S(2)}, u32[]{:S(2)}) async-start(bf16[3072,2,2048]{0,2,1:T(8,128)(2,1)} %bitcast.36), calls=%async_computation.1 | async-start | bytes 50331648 | tf_op jit(solution)/shard_map/all_to_all | solution.py:27
  336.5 414.1 %all-reduce.3.cloned.1.call-start = ((), (), s32[]{:S(2)}) async-start(), calls=%async_computation.5 | async-start | bytes 589824
  687.3 128.5 %copy-start.1 = (bf16[16,6144]{1,0:T(8,128)(2,1)S(1)}, bf16[16,6144]{1,0:T(8,128)(2,1)}, u32[]{:S(2)}) copy-start(bf16[16,6144]{1,0:T(8,128)(2,1)} %param.6) | copy-start | bytes 589828
  752.8 7.5 all-to-all-start.2
  756.1 58.3 %reduce-scatter.2.cloned.1.call-start = ((), (), s32[]{:S(2)}) async-start(), calls=%async_computation.4 | async-start | bytes 417792 | tf_op jit(solution)/shard_map/reduce_scatter | solution.py:50
Sparse Core Ops, SparseCore 0:
  714.2 36.3 all-reduce.2
  761.7 52.6 reduce-scatter.1
where the time goes:
time: 826 us; the launch traced here: 823 us
  waiting for transfers between devices  334 us (40%)
  blocking collectives  281 us (34%)
  local copies, waits for them, and re-layouts  133 us (16%)
  matrix products  32.7 us (4%)
  starting transfers between devices  27.1 us (3%)
  between operations  13.5 us (2%)
    all_gather x1, blocking collectives, per_device(): piece = lax.all_gather(outgoing, 'gy', axis=0, tiled=True)  275 us
    all_to_all x1, waiting for transfers between devices, per_device(): lax.all_to_all(w_gate[0], 'gy', split_axis=1, concat_axis=0, tiled=True)  241 us
    unnamed x16, local copies, waits for them, and re-layouts  67.6 us
    reduce_scatter x1, waiting for transfers between devices, per_device(): lax.psum_scatter(contribution, ('gx', 'gz'), scatter_dimension=1, tiled=T...  52.8 us
    unnamed x3, waiting for transfers between devices  36.5 us
    all_to_all x1, local copies, waits for them, and re-layouts, per_device(): lax.all_to_all(w_up[0], 'gy', split_axis=1, concat_axis=0, tiled=True)  32.7 us
    all_to_all x1, local copies, waits for them, and re-layouts, per_device(): lax.all_to_all(w_gate[0], 'gy', split_axis=1, concat_axis=0, tiled=True)  31.6 us
  transfers between devices with their start and end apart: 5, of which 4 were waited for; matrix products, arithmetic and copies ran while one was open for 8% of the time, Pallas kernels for 0%

commit v1 on v0

--- a/solution.py
+++ b/solution.py
@@ -22,14 +22,14 @@
     shares = weights_f / jnp.sum(weights_f, axis=1, keepdims=True)
     token_gate = jnp.sum(hits.astype(jnp.float32) * shares, axis=1)
     slot_gate = jnp.dot(place_full, token_gate, precision=lax.Precision.HIGHEST)
-    gate_slab, up_slab = (
-        lax.all_to_all(w_gate[0], "gy", split_axis=1, concat_axis=0, tiled=True),
-        lax.all_to_all(w_up[0], "gy", split_axis=1, concat_axis=0, tiled=True),
-    )
-    piece = lax.all_gather(outgoing, "gy", axis=0, tiled=True)
-    gate = jnp.dot(piece, gate_slab, preferred_element_type=jnp.float32)
-    upper = jnp.dot(piece, up_slab, preferred_element_type=jnp.float32)
-    hidden = (jax.nn.silu(gate) * upper).astype(jnp.bfloat16)
+    depth = w_gate.shape[1]
+    half = outgoing.reshape(CAP, owners, depth).transpose(1, 0, 2)
+    piece = lax.all_to_all(half, "gy", split_axis=0, concat_axis=0, tiled=True)
+    piece = piece.reshape(owners * CAP, depth)
+    gate = jnp.dot(piece, w_gate[0], preferred_element_type=jnp.float32)
+    upper = jnp.dot(piece, w_up[0], preferred_element_type=jnp.float32)
+    both = lax.psum_scatter(jnp.stack([gate, upper]), "gy", scatter_dimension=2, tiled=True)
+    hidden = (jax.nn.silu(both[0]) * both[1]).astype(jnp.bfloat16)
     down_local = w_down[0]
     partial_value = jnp.dot(
         lax.all_gather(hidden, "gy", axis=1, tiled=True),

time: 826 us -> 182 us (0.22)
  blocking collectives: 281 us -> 14.1 us
  waiting for transfers between devices: 334 us -> 110 us
  local copies, waits for them, and re-layouts: 133 us -> 3.36 us
  starting transfers between devices: 27.1 us -> 3.39 us
    all_gather x1 -> x0, blocking collectives: 275 us -> none  [per_device(): piece = lax.all_gather(outgoing, 'gy', axis=0, tiled=True)]
    all_to_all x2 -> x0, waiting for transfers between devices: 241 us -> none  [the longest x1 241 us: per_device(): lax.all_to_all(w_gate[0], 'gy', split_axis=1, concat_axis=0, tiled=True)]
    unnamed x16 -> x13, local copies, waits for them, and re-layouts: 67.6 us -> 2.19 us
    all_to_all x2 -> x0, local copies, waits for them, and re-layouts: 64.3 us -> none  [the longest x1 32.7 us: per_device(): lax.all_to_all(w_up[0], 'gy', split_axis=1, concat_axis=0, tiled=True)]
    all_to_all x2 -> x0, starting transfers between devices: 23.8 us -> none  [the longest x1 11.9 us: per_device(): lax.all_to_all(w_up[0], 'gy', split_axis=1, concat_axis=0, tiled=True)]
    reduce_scatter x0 -> x1, waiting for transfers between devices: none -> 17.3 us  [per_device(): lax.psum_scatter(jnp.stack([gate, upper]), 'gy', scatter_dimension=2, til...]
    all_to_all x0 -> x1, blocking collectives: none -> 8.86 us  [per_device(): piece = lax.all_to_all(half, 'gy', split_axis=0, concat_axis=0, tiled=True)]
    unnamed x3 -> x4, waiting for transfers between devices: 36.5 us -> 36.1 us
  transfers between devices with their start and end apart: 5 -> 4, of which waited for: 4 -> 4; matrix products, arithmetic and copies ran while one was open for 8% -> 0% of each run, Pallas kernels for 0% -> 0%
where the time goes in v1:
time: 182 us; the launch traced here: 181 us
  waiting for transfers between devices  110 us (60%)
  matrix products  32.7 us (18%)
  blocking collectives  14.1 us (8%)
  between operations  13.2 us (7%)
  other arithmetic  4.3 us (2%)
  starting transfers between devices  3.39 us (2%)
  local copies, waits for them, and re-layouts  3.36 us (2%)
    reduce_scatter x1, waiting for transfers between devices, per_device(): lax.psum_scatter(contribution, ('gx', 'gz'), scatter_dimension=1, tiled=T...  52.8 us
    unnamed x4, waiting for transfers between devices  36.1 us
    reduce_scatter x1, waiting for transfers between devices, per_device(): lax.psum_scatter(jnp.stack([gate, upper]), 'gy', scatter_dimension=2, til...  17.3 us
    dot_general x1, matrix products, per_device(): jnp.dot(lax.all_gather(hidden, 'gy', axis=1, tiled=True), down_local, pre...  11.3 us
    dot_general x1, matrix products, per_device(): upper = jnp.dot(piece, w_up[0], preferred_element_type=jnp.float32)  10 us
    dot_general x1, matrix products, per_device(): gate = jnp.dot(piece, w_gate[0], preferred_element_type=jnp.float32)  9.9 us
    all_to_all x1, blocking collectives, per_device(): piece = lax.all_to_all(half, 'gy', split_axis=0, concat_axis=0, tiled=True)  8.86 us
    all_gather x1, blocking collectives, per_device(): lax.all_gather(hidden, 'gy', axis=1, tiled=True)  5.29 us
  transfers between devices with their start and end apart: 4, of which 4 were waited for; matrix products, arithmetic and copies ran while one was open for 0% of the time, Pallas kernels for 0%

profile of v1, /device:TPU:0, one launch (start us, length us, event | category | flops | bytes accessed | tf_op | source)
XLA Modules:
  0.0 181.3 jit_solution(7835118890817340249)
XLA Ops:
  6.5 0.0 copy-start
  6.5 0.0 reduce-scatter.3.cloned.1.call-start
  6.5 0.7 fusion.21
  7.3 0.1 copy.23
  7.4 0.1 add_reduce_fusion
  7.5 0.0 copy-done
  7.5 0.2 convolution_convert_fusion
  7.7 0.1 reshape.49
  7.9 8.9 %all_to_all.14 = bf16[2,12,3072]{2,1,0:T(8,128)(2,1)S(1)} all-to-all(bf16[2,12,3072]{2,1,0:T(8,128)(2,1)S(1)} %bitcast.51), channel_id=1, replica_groups=mesh['gx'=4,'gy'=2,'gz'=4] {'gy'}, dimensions={0} | all-to-all | bytes 294912 | tf_op jit(solution)/shard_map/all_to_all | solution.py:27
  16.8 9.9 %fusion.6 = f32[1,24,4096]{2,1,0:T(8,128)S(1)} fusion(bf16[24,3072]{1,0:T(8,128)(2,1)S(1)} %reshape.50, bf16[1,3072,4096]{2,1,0:T(8,128)(2,1)} %param.9), kind=kOutput, calls=%fused_computation.7 | convolution fusion | flops 603979776 | bytes 25706496 | tf_op jit(solution)/shard_map/dot_general | solution.py:29
  26.7 0.0 copy-start.4
  26.7 0.0 copy-start.3
  26.7 0.0 copy-start.1
  26.7 10.0 %fusion.9 = f32[1,24,4096]{2,1,0:T(8,128)S(1)} fusion(bf16[24,3072]{1,0:T(8,128)(2,1)S(1)} %reshape.50, bf16[1,3072,4096]{2,1,0:T(8,128)(2,1)} %param.10), kind=kOutput, calls=%fused_computation.8 | convolution fusion | flops 603979776 | bytes 25706496 | tf_op jit(solution)/shard_map/dot_general | solution.py:30
  36.7 0.0 copy-start.2
  36.7 0.9 pad_maximum_fusion
  37.6 0.0 reduce-scatter.3.cloned.1.call-update
  37.6 0.0 all-reduce.3.cloned.1.call-start
  37.7 0.0 copy-done.4
  37.7 0.6 dynamic-slice
  38.3 0.0 copy-done.3
  38.3 17.3 %reduce-scatter.3.cloned.1.call-done = f32[2,24,2048]{2,1,0:T(8,128)} async-done(((f32[2,24,4096]{2,1,0:T(8,128)}), f32[2,24,2048]{2,1,0:T(8,128)}) %reduce-scatter.3.cloned.1.call-update) | async-done | bytes 393232 | tf_op jit(solution)/shard_map/reduce_scatter | solution.py:31
  55.6 1.1 fusion.13
  56.7 5.3 %all_gather.3 = bf16[24,4096]{1,0:T(8,128)(2,1)S(1)} all-gather(bf16[24,2048]{1,0:T(8,128)(2,1)S(1)} %fusion.13), channel_id=1, replica_groups=mesh['gx'=4,'gy'=2,'gz'=4] {'gy'}, dimensions={1}, use_global_device_ids=true | all-gather | bytes 294912 | tf_op jit(solution)/shard_map/all_gather | solution.py:35
  62.0 0.1 dot_general.24
  62.1 11.3 %fusion = f32[2,4,3,3072]{3,0,2,1:T(2,128)} fusion(bf16[1,4096,3072]{2,1,0:T(8,128)(2,1)} %param.11, bf16[2,4,3,4096]{3,2,1,0:T(4,128)(2,1)S(1)} %dot_general.24), kind=kOutput, calls=%fused_computation | convolution fusion | flops 603979776 | bytes 25657344 | tf_op jit(solution)/shard_map/dot_general | solution.py:34
  73.4 0.0 all-reduce.3.cloned.1.call-update
  73.5 0.0 copy-done.2
  73.5 36.1 %all-reduce.3.cloned.1.call-done = f32[2,4,3,3072]{3,0,2,1:T(2,128)} async-done(((f32[2,4,3,3072]{3,0,2,1:T(2,128)}), f32[2,4,3,3072]{3,0,2,1:T(2,128)}) %all-reduce.3.cloned.1.call-update) | async-done | bytes 294928
  109.6 1.5 constant_dynamic-slice_fusion
  111.1 0.7 copy.27
  111.8 3.3 %all-to-all-start.1 = ((f32[2,1,3,3072]{3,1,2,0:T(1,128)}), f32[2,1,3,3072]{3,1,2,0:T(1,128)S(1)}, u32[]{:S(2)}, u32[]{:S(2)}) async-start(f32[2,1,3,3072]{3,1,2,0:T(1,128)} %copy.27), calls=%async_computation.2 | async-start | bytes 147456 | tf_op jit(solution)/shard_map/all_to_all | solution.py:43
  115.1 0.0 reduce-scatter.5.cloned.1.call-start
  115.2 0.1 convolution_bitcast_fusion
  115.3 0.1 dynamic_slice.7
  115.4 3.9 %all-to-all-done.1 = f32[2,1,3,3072]{3,1,2,0:T(1,128)S(1)} async-done(((f32[2,1,3,3072]{3,1,2,0:T(1,128)}), f32[2,1,3,3072]{3,1,2,0:T(1,128)S(1)}, u32[]{:S(2)}, u32[]{:S(2)}) %all-to-all-start.1) | async-done | bytes 73760 | tf_op jit(solution)/shard_map/all_to_all | solution.py:43
  119.4 1.2 fusion.15
  120.6 0.0 reduce-scatter.5.cloned.1.call-update
  120.6 52.8 %reduce-scatter.5.cloned.1.call-done = f32[16,384]{1,0:T(8,128)} async-done(((f32[16,6144]{1,0:T(8,128)}), f32[16,384]{1,0:T(8,128)}) %reduce-scatter.5.cloned.1.call-update) | async-done | bytes 24592 | tf_op jit(solution)/shard_map/reduce_scatter | solution.py:50
  173.4 1.3 convert_element_type.25
  174.8 0.0 copy-done.1
  (9 shorter events, 0.2 us)
Async XLA Ops:
  6.5 1.0 copy-start
  6.5 49.1 %reduce-scatter.3.cloned.1.call-start = ((), (), s32[]{:S(2)}) async-start(), calls=%async_computation.4 | async-start | bytes 1179648 | tf_op jit(solution)/shard_map/reduce_scatter | solution.py:31
  26.7 11.0 %copy-start.4 = (u32[32]{0:T(128)S(1)}, u32[32]{0:T(128)}, u32[]{:S(2)}) copy-start(u32[32]{0:T(128)} %constant.30) | copy-start | bytes 388
  26.7 11.6 %copy-start.3 = (s32[16,2]{0,1:T(2,128)S(1)}, s32[16,2]{0,1:T(2,128)}, u32[]{:S(2)}) copy-start(s32[16,2]{0,1:T(2,128)} %param.8) | copy-start | bytes 388
  26.7 148.1 %copy-start.1 = (bf16[16,6144]{1,0:T(8,128)(2,1)S(1)}, bf16[16,6144]{1,0:T(8,128)(2,1)}, u32[]{:S(2)}) copy-start(bf16[16,6144]{1,0:T(8,128)(2,1)} %param.6) | copy-start | bytes 589828
  36.7 36.8 %copy-start.2 = (s32[16,2]{0,1:T(2,128)S(1)}, s32[16,2]{0,1:T(2,128)}, u32[]{:S(2)}) copy-start(s32[16,2]{0,1:T(2,128)} %param.7) | copy-start | bytes 388
  37.6 71.9 %all-reduce.3.cloned.1.call-start = ((), (), s32[]{:S(2)}) async-start(), calls=%async_computation.6 | async-start | bytes 589824
  111.8 7.5 %all-to-all-start.1 = ((f32[2,1,3,3072]{3,1,2,0:T(1,128)}), f32[2,1,3,3072]{3,1,2,0:T(1,128)S(1)}, u32[]{:S(2)}, u32[]{:S(2)}) async-start(f32[2,1,3,3072]{3,1,2,0:T(1,128)} %copy.27), calls=%async_computation.2 | async-start | bytes 147456 | tf_op jit(solution)/shard_map/all_to_all | solution.py:43
  115.1 58.3 %reduce-scatter.5.cloned.1.call-start = ((), (), s32[]{:S(2)}) async-start(), calls=%async_computation.5 | async-start | bytes 417792 | tf_op jit(solution)/shard_map/reduce_scatter | solution.py:50
Sparse Core Ops, SparseCore 0:
  37.8 17.8 reduce-scatter.2
  73.6 35.9 all-reduce.2
  120.7 52.6 reduce-scatter.4
